TPU v7x, 32 devices: a whole 2x2x4 slice. The times are simulated.
32 devices in a mesh: gx: 4 (over z), gy: 2 (over x), gz: 4 (over y, core).
Axes of the slice: x: 2, y: 2, z: 4, core: 2. Of those that a mesh axis runs over, the one named last changes fastest.
Arguments:
- images: float32 [2, 64, 64, 512], P(None, 'gx', 'gy', 'gz'), may hold values from -6 to 6
- velocity: float32 [2, 3, 8, 8, 64], P(None, None, 'gx', None, 'gz'), may hold values from -2 to 2
Outputs:
- new_velocity: float32 [2, 3, 8, 8, 64], P(None, None, 'gx', None, 'gz')
- velocity_field: bfloat16 [2, 3, 64, 64, 512], P(None, None, 'gx', 'gy', 'gz')
All inputs are finite; a program needn't handle non-finite values.
Results may differ from a plain program's by a relative error of at most 0.001.
Values sent between devices are 32-bit elements; how exact they have to be, the bound alone decides.
A program may use at most 64 MiB of HBM per device.

v0:
```python
import jax
import jax.numpy as jnp
from jax import lax
from jax.sharding import PartitionSpec as P

epsilon_value = 1e-05
step_size = 0.5


def extended_2(cells, sides, width):
    for axis, dim in sides:
        count = lax.axis_size(axis)
        ends = count - 1
        head = lax.slice_in_dim(cells, 0, width, axis=dim)
        tail = lax.slice_in_dim(cells, cells.shape[dim] - width, cells.shape[dim], axis=dim)
        cells = jnp.concatenate(
            [
                lax.ppermute(tail, axis, [(i, (i + 1) % count) for i in range(ends)]),
                cells,
                lax.ppermute(head, axis, [((i + 1) % count, i) for i in range(ends)]),
            ],
            axis=dim,
        )
    return cells


def spline_weight(offset):
    magnitude = jnp.abs(offset)
    interior = 2.0 / 3.0 - magnitude * magnitude + 0.5 * magnitude * magnitude * magnitude
    outside = jnp.maximum(2.0 - magnitude, 0.0)
    outside = outside * outside * outside / 6.0
    return jnp.where(magnitude < 1.0, interior, outside)


def spline_table(voxels, points, first_point):
    positions = jnp.arange(voxels, dtype=jnp.float32)[:, None]
    centres = 8.0 * (jnp.arange(points, dtype=jnp.float32)[None, :] + first_point) + 3.5
    return spline_weight((positions - centres) / 8.0)


def fold_matrix(length):
    table_rows = jnp.arange(length, dtype=jnp.int32)[:, None]
    columns = jnp.arange(length - 8, dtype=jnp.int32)[None, :]
    matches = (
        (table_rows == columns + 4)
        | (table_rows < 2) & (columns == table_rows)
        | (table_rows >= length - 2) & (columns == table_rows - 8)
    )
    return matches.astype(jnp.float32)


def window_sum(values, which_axis, keep_count):
    running = lax.slice_in_dim(values, 0, keep_count, axis=which_axis)
    for offset in range(1, 9):
        running = running + lax.slice_in_dim(values, offset, offset + keep_count, axis=which_axis)
    return running


def gradient(volume, count_x, count_y, count_z):
    along_x = (
        volume[5 : 5 + count_x, 4 : 4 + count_y, 4 : 4 + count_z]
        - volume[3 : 3 + count_x, 4 : 4 + count_y, 4 : 4 + count_z]
    )
    along_y = (
        volume[4 : 4 + count_x, 5 : 5 + count_y, 4 : 4 + count_z]
        - volume[4 : 4 + count_x, 3 : 3 + count_y, 4 : 4 + count_z]
    )
    along_z = (
        volume[4 : 4 + count_x, 4 : 4 + count_y, 5 : 5 + count_z]
        - volume[4 : 4 + count_x, 4 : 4 + count_y, 3 : 3 + count_z]
    )
    return 0.5 * jnp.stack([along_x, along_y, along_z])


def local_forces(padded):
    count_x = padded.shape[1] - 8
    count_y = padded.shape[2] - 8
    count_z = padded.shape[3] - 8
    fixed_side = padded[0]
    moving_side = padded[1]
    products = jnp.stack(
        [
            fixed_side,
            moving_side,
            fixed_side * fixed_side,
            moving_side * moving_side,
            fixed_side * moving_side,
        ]
    )
    window_sums = window_sum(window_sum(window_sum(products, 1, count_x), 2, count_y), 3, count_z)
    averages = window_sums / 729.0
    mean_fixed = averages[0]
    mean_moving = averages[1]
    var_fixed = averages[2] - mean_fixed * mean_fixed + epsilon_value
    var_moving = averages[3] - mean_moving * mean_moving + epsilon_value
    covariance = averages[4] - mean_fixed * mean_moving
    centre_fixed = fixed_side[4 : 4 + count_x, 4 : 4 + count_y, 4 : 4 + count_z] - mean_fixed
    centre_moving = moving_side[4 : 4 + count_x, 4 : 4 + count_y, 4 : 4 + count_z] - mean_moving
    factor = 2.0 * covariance / (var_fixed * var_moving)
    pull_fixed = factor * (centre_moving - covariance / var_fixed * centre_fixed)
    pull_moving = factor * (centre_fixed - covariance / var_moving * centre_moving)
    return jnp.stack(
        [
            pull_fixed[None] * gradient(fixed_side, count_x, count_y, count_z),
            pull_moving[None] * gradient(moving_side, count_x, count_y, count_z),
        ]
    )


def shards(images, velocity):
    highest = lax.Precision.HIGHEST
    count_x = images.shape[1]
    count_y = images.shape[2]
    count_z = images.shape[3]
    block_x = count_x // 8
    block_y = count_y // 8
    block_z = count_z // 8
    padded = extended_2(images, (("gx", 1), ("gy", 2), ("gz", 3)), 4)
    pushes = local_forces(padded)
    table_x = spline_table(count_x, block_x + 4, -2.0)
    table_y = spline_table(count_y, block_y + 4, -2.0)
    table_z = spline_table(count_z, block_z + 4, -2.0)
    along_z = jnp.einsum("hcxyz,zk->hcxyk", pushes, table_z, precision=highest)
    along_y = jnp.einsum("hcxyk,yj->hcxjk", along_z, table_y, precision=highest)
    partial_value = jnp.einsum("hcxjk,xi->hcijk", along_y, table_x, precision=highest)
    fold_x = fold_matrix(block_x + 8)
    fold_z = fold_matrix(block_z + 8)
    extended = extended_2(partial_value, (("gx", 2), ("gz", 4)), 2)
    folded = jnp.einsum("hcpqr,pi->hciqr", extended, fold_x, precision=highest)
    folded = jnp.einsum("hciqr,rk->hciqk", folded, fold_z, precision=highest)
    whole_rows = block_y * lax.axis_size("gy") + 4
    canvas = jnp.zeros((2, 3, block_x, whole_rows, block_z), jnp.float32)
    canvas = lax.dynamic_update_slice_in_dim(canvas, folded, lax.axis_index("gy") * block_y, 3)
    summed = lax.psum(canvas, "gy")
    descent = summed[:, :, :, 2 : whole_rows - 2, :]
    new_velocity = velocity + step_size * descent
    beside_all = extended_2(new_velocity, (("gx", 2), ("gz", 4)), 2)
    rows_padded = jnp.pad(beside_all, ((0, 0), (0, 0), (0, 0), (2, 2), (0, 0)))
    window = lax.dynamic_slice_in_dim(rows_padded, lax.axis_index("gy") * block_y, block_y + 4, 3)
    field_x = jnp.einsum("hcijk,xi->hcxjk", window, table_x, precision=highest)
    field_y = jnp.einsum("hcxjk,yj->hcxyk", field_x, table_y, precision=highest)
    velocity_field = jnp.einsum("hcxyk,zk->hcxyz", field_y, table_z, precision=highest).astype(
        jnp.bfloat16
    )
    return (new_velocity, velocity_field)


def solution(mesh):
    placed = (P(None, "gx", "gy", "gz"), P(None, None, "gx", None, "gz"))
    return jax.shard_map(
        shards,
        mesh=mesh,
        in_specs=placed,
        out_specs=(P(None, None, "gx", None, "gz"), P(None, None, "gx", "gy", "gz")),
        check_vma=False,
    )
```

profile of v0, /device:TPU:1, one launch (start us, length us, event | category | flops | bytes accessed | tf_op | source)
XLA Modules:
  0.0 113.0 jit_solution(16727576706066880578)
XLA Ops:
  1.6 4.0 %collective-permute-start = (f32[2,4,32,128]{3,2,1,0:T(8,128)S(1)}, f32[2,4,32,128]{3,2,1,0:T(8,128)S(1)}, u32[]{:S(2)}, u32[]{:S(2)}) collective-permute-start(f32[2,4,32,128]{3,2,1,0:T(8,128)S(1)} %get-tuple-element.25), channel_id=1, source_target_pairs={{0,8},{8,16},{16,24},{1,9},{9,17},{17,25},{2,10},{10,18},{18,26},{... | collective-permute-start | bytes 393224 | tf_op jit(solution)/shard_map/ppermute | solution.py:18
  5.7 1.3 %collective-permute-start.1 = (f32[2,4,32,128]{3,2,1,0:T(8,128)S(1)}, f32[2,4,32,128]{3,2,1,0:T(8,128)S(1)}, u32[]{:S(2)}, u32[]{:S(2)}) collective-permute-start(f32[2,4,32,128]{3,2,1,0:T(8,128)S(1)} %get-tuple-element.24), channel_id=1, source_target_pairs={{8,0},{16,8},{24,16},{9,1},{17,9},{25,17},{10,2},{18,10},{26,18},{... | collective-permute-start | bytes 393224 | tf_op jit(solution)/shard_map/ppermute | solution.py:20
  7.8 1.1 constant_dynamic-update-slice_fusion.1
  8.9 2.5 %collective-permute-done.1 = f32[2,4,32,128]{3,2,1,0:T(8,128)S(1)} collective-permute-done((f32[2,4,32,128]{3,2,1,0:T(8,128)S(1)}, f32[2,4,32,128]{3,2,1,0:T(8,128)S(1)}, u32[]{:S(2)}, u32[]{:S(2)}) %collective-permute-start.1) | collective-permute-done | bytes 131104 | tf_op jit(solution)/shard_map/ppermute | solution.py:20
  11.4 3.1 %collective-permute-start.2 = (f32[2,24,4,128]{3,1,2,0:T(8,128)S(1)}, f32[2,24,4,128]{3,1,2,0:T(8,128)S(1)}, u32[]{:S(2)}, u32[]{:S(2)}) collective-permute-start(f32[2,24,4,128]{3,1,2,0:T(8,128)S(1)} %copy.59), channel_id=1, source_target_pairs={{0,4},{1,5},{2,6},{3,7},{8,12},{9,13},{10,14},{11,15},{16,20},{17,... | collective-permute-start | bytes 294920 | tf_op jit(solution)/shard_map/ppermute | solution.py:18
  14.6 1.3 %collective-permute-start.3 = (f32[2,24,4,128]{3,1,2,0:T(8,128)S(1)}, f32[2,24,4,128]{3,1,2,0:T(8,128)S(1)}, u32[]{:S(2)}, u32[]{:S(2)}) collective-permute-start(f32[2,24,4,128]{3,1,2,0:T(8,128)S(1)} %copy.60), channel_id=1, source_target_pairs={{4,0},{5,1},{6,2},{7,3},{12,8},{13,9},{14,10},{15,11},{20,16},{21,... | collective-permute-start | bytes 294920 | tf_op jit(solution)/shard_map/ppermute | solution.py:20
  16.2 3.7 %collective-permute-done.3 = f32[2,24,4,128]{3,1,2,0:T(8,128)S(1)} collective-permute-done((f32[2,24,4,128]{3,1,2,0:T(8,128)S(1)}, f32[2,24,4,128]{3,1,2,0:T(8,128)S(1)}, u32[]{:S(2)}, u32[]{:S(2)}) %collective-permute-start.3) | collective-permute-done | bytes 98336 | tf_op jit(solution)/shard_map/ppermute | solution.py:20
  20.8 6.6 %collective-permute-start.4 = (f32[2,24,40,4]{2,1,3,0:T(8,128)S(1)}, f32[2,24,40,4]{2,1,3,0:T(8,128)S(1)}, u32[]{:S(2)}, u32[]{:S(2)}) collective-permute-start(f32[2,24,40,4]{2,1,3,0:T(8,128)S(1)} %copy.44), channel_id=1, source_target_pairs={{0,1},{1,2},{2,3},{4,5},{5,6},{6,7},{8,9},{9,10},{10,11},{12,13},{... | collective-permute-start | bytes 92168 | tf_op jit(solution)/shard_map/ppermute | solution.py:18
  27.8 1.9 %collective-permute-start.5 = (f32[2,24,40,4]{2,1,3,0:T(8,128)S(1)}, f32[2,24,40,4]{2,1,3,0:T(8,128)S(1)}, u32[]{:S(2)}, u32[]{:S(2)}) collective-permute-start(f32[2,24,40,4]{2,1,3,0:T(8,128)S(1)} %copy.45), channel_id=1, source_target_pairs={{1,0},{2,1},{3,2},{5,4},{6,5},{7,6},{9,8},{10,9},{11,10},{13,12},{... | collective-permute-start | bytes 92168 | tf_op jit(solution)/shard_map/ppermute | solution.py:20
  30.2 3.6 %collective-permute-done.5 = f32[2,24,40,4]{2,1,3,0:T(8,128)S(1)} collective-permute-done((f32[2,24,40,4]{2,1,3,0:T(8,128)S(1)}, f32[2,24,40,4]{2,1,3,0:T(8,128)S(1)}, u32[]{:S(2)}, u32[]{:S(2)}) %collective-permute-start.5) | collective-permute-done | bytes 30752 | tf_op jit(solution)/shard_map/ppermute | solution.py:20
  35.6 1.8 %pad_maximum_fusion = f32[5,24,40,136]{3,2,1,0:T(8,128)S(1)} fusion(f32[1,24,40,136]{3,2,1,0:T(8,128)S(1)} %get-tuple-element.12, f32[1,24,40,136]{3,2,1,0:T(8,128)S(1)} %get-tuple-element.14, f32[1,24,40,136]{3,2,1,0:T(8,128)S(1)} %get-tuple-element.11, f32[2,24,40,4]{3,2,1,0:T(8,128)S(1)} %copy.47, f32[2,24,4,128]{3,2,1,0:T(4,128)S(1)} %copy.43, ...), kind=kLoop, calls=%fused_computation | loop fusion | flops 4569600 | bytes 5222400 | tf_op jit(solution)/shard_map/stack | solution.py:81
  37.4 3.0 %slice_add_fusion = f32[5,16,40,136]{3,2,1,0:T(8,128)S(1)} fusion(f32[5,24,40,136]{3,2,1,0:T(8,128)S(1)} %pad_maximum_fusion), kind=kLoop, calls=%fused_computation.1 | loop fusion | flops 3481600 | bytes 17408000 | tf_op jit(solution)/shard_map/add | solution.py:55
  40.5 2.0 %slice_add_fusion.8 = f32[5,16,32,136]{3,2,1,0:T(8,128)S(1)} fusion(f32[5,16,40,136]{3,2,1,0:T(8,128)S(1)} %slice_add_fusion), kind=kLoop, calls=%fused_computation.9 | loop fusion | flops 2785280 | bytes 13926400 | tf_op jit(solution)/shard_map/add | solution.py:55
  42.4 2.8 %fusion.4 = f32[5,16,32,128]{3,2,1,0:T(8,128)S(1)} fusion(f32[5,16,32,136]{3,2,1,0:T(8,128)S(1)} %slice_add_fusion.8), kind=kLoop, calls=%fused_computation.25 | loop fusion | flops 2949120 | bytes 13107200 | tf_op jit(solution)/shard_map/div | solution.py:91
  46.5 6.2 %fusion = f32[2,3,16,32,20]{3,4,2,1,0:T(8,128)S(1)} fusion(f32[1,3,16,32,128]{4,3,2,1,0:T(8,128)S(1)} %maximum_multiply_fusion.1, f32[1,3,16,32,128]{4,3,2,1,0:T(8,128)S(1)} %maximum_multiply_fusion, f32[20]{0:T(128)S(1)} %multiply_add_fusion), kind=kOutput, calls=%fused_computation.18 | convolution fusion | flops 94806016 | bytes 1818704 | tf_op jit(solution)/shard_map/hcxyz,zk->hcxyk/dot_general | solution.py:123
  52.7 5.9 %convolution_bitcast_fusion.2 = f32[2,3,16,8,20]{4,3,2,1,0:T(8,128)S(1)} fusion(f32[2,3,16,32,20]{3,4,2,1,0:T(8,128)S(1)} %fusion, f32[8]{0:T(128)S(1)} %multiply_add_fusion.1), kind=kOutput, calls=%fused_computation.34 | convolution fusion | flops 5902336 | bytes 307232 | tf_op jit(solution)/shard_map/hcxyk,yj->hcxjk/dot_general | solution.py:124
  59.1 3.2 %collective-permute-start.6 = (f32[2,3,2,8,20]{4,2,3,1,0:T(2,128)S(1)}, f32[2,3,2,8,20]{4,2,3,1,0:T(2,128)S(1)}, u32[]{:S(2)}, u32[]{:S(2)}) collective-permute-start(f32[2,3,2,8,20]{4,2,3,1,0:T(2,128)S(1)} %get-tuple-element.30), channel_id=1, source_target_pairs={{0,8},{8,16},{16,24},{1,9},{9,17},{17,25},{2,10},{10,18},{18,26},{... | collective-permute-start | bytes 23048 | tf_op jit(solution)/shard_map/ppermute | solution.py:18
  62.3 1.5 %collective-permute-start.7 = (f32[2,3,2,8,20]{4,2,3,1,0:T(2,128)S(1)}, f32[2,3,2,8,20]{4,2,3,1,0:T(2,128)S(1)}, u32[]{:S(2)}, u32[]{:S(2)}) collective-permute-start(f32[2,3,2,8,20]{4,2,3,1,0:T(2,128)S(1)} %get-tuple-element.31), channel_id=1, source_target_pairs={{8,0},{16,8},{24,16},{9,1},{17,9},{25,17},{10,2},{18,10},{26,18},{... | collective-permute-start | bytes 23048 | tf_op jit(solution)/shard_map/ppermute | solution.py:20
  63.8 3.3 %collective-permute-done.7 = f32[2,3,2,8,20]{4,2,3,1,0:T(2,128)S(1)} collective-permute-done((f32[2,3,2,8,20]{4,2,3,1,0:T(2,128)S(1)}, f32[2,3,2,8,20]{4,2,3,1,0:T(2,128)S(1)}, u32[]{:S(2)}, u32[]{:S(2)}) %collective-permute-start.7) | collective-permute-done | bytes 7712 | tf_op jit(solution)/shard_map/ppermute | solution.py:20
  67.4 3.3 %collective-permute-start.8 = (f32[2,3,10,8,2]{4,2,3,1,0:T(8,128)S(1)}, f32[2,3,10,8,2]{4,2,3,1,0:T(8,128)S(1)}, u32[]{:S(2)}, u32[]{:S(2)}) collective-permute-start(f32[2,3,10,8,2]{4,2,3,1,0:T(8,128)S(1)} %get-tuple-element.26), channel_id=1, source_target_pairs={{0,1},{1,2},{2,3},{4,5},{5,6},{6,7},{8,9},{9,10},{10,11},{12,13},{... | collective-permute-start | bytes 11528 | tf_op jit(solution)/shard_map/ppermute | solution.py:18
  70.6 1.9 %collective-permute-start.9 = (f32[2,3,10,8,2]{4,2,3,1,0:T(8,128)S(1)}, f32[2,3,10,8,2]{4,2,3,1,0:T(8,128)S(1)}, u32[]{:S(2)}, u32[]{:S(2)}) collective-permute-start(f32[2,3,10,8,2]{4,2,3,1,0:T(8,128)S(1)} %get-tuple-element.27), channel_id=1, source_target_pairs={{1,0},{2,1},{3,2},{5,4},{6,5},{7,6},{9,8},{10,9},{11,10},{13,12},{... | collective-permute-start | bytes 11528 | tf_op jit(solution)/shard_map/ppermute | solution.py:20
  72.6 2.8 %collective-permute-done.8 = f32[2,3,10,8,2]{4,2,3,1,0:T(8,128)S(1)} collective-permute-done((f32[2,3,10,8,2]{4,2,3,1,0:T(8,128)S(1)}, f32[2,3,10,8,2]{4,2,3,1,0:T(8,128)S(1)}, u32[]{:S(2)}, u32[]{:S(2)}) %collective-permute-start.8) | collective-permute-done | bytes 3872 | tf_op jit(solution)/shard_map/ppermute | solution.py:18
  75.3 4.7 %collective-permute-done.9 = f32[2,3,10,8,2]{4,2,3,1,0:T(8,128)S(1)} collective-permute-done((f32[2,3,10,8,2]{4,2,3,1,0:T(8,128)S(1)}, f32[2,3,10,8,2]{4,2,3,1,0:T(8,128)S(1)}, u32[]{:S(2)}, u32[]{:S(2)}) %collective-permute-start.9) | collective-permute-done | bytes 3872 | tf_op jit(solution)/shard_map/ppermute | solution.py:20
  80.9 5.6 %psum.7 = f32[2,3,2,12,16]{4,2,3,1,0:T(2,128)S(1)} all-reduce(f32[2,3,2,12,16]{4,2,3,1,0:T(2,128)S(1)} %copy_dynamic-update-slice_fusion), channel_id=1, replica_groups=mesh['gx'=4,'gy'=2,'gz'=4] {'gy'}, use_global_device_ids=true, to_apply=%region_0.1 | all-reduce | flops 2304 | bytes 18432 | tf_op jit(solution)/shard_map/psum | solution.py:134
  86.6 3.2 %collective-permute-start.10 = (f32[2,3,2,8,16]{4,2,3,1,0:T(2,128)S(1)}, f32[2,3,2,8,16]{4,2,3,1,0:T(2,128)S(1)}, u32[]{:S(2)}, u32[]{:S(2)}) collective-permute-start(f32[2,3,2,8,16]{4,2,3,1,0:T(2,128)S(1)} %fusion.51), channel_id=1, source_target_pairs={{0,8},{8,16},{16,24},{1,9},{9,17},{17,25},{2,10},{10,18},{18,26},{... | collective-permute-start | bytes 18440 | tf_op jit(solution)/shard_map/ppermute | solution.py:18
  89.8 1.3 %collective-permute-start.11 = (f32[2,3,2,8,16]{4,2,3,1,0:T(2,128)S(1)}, f32[2,3,2,8,16]{4,2,3,1,0:T(2,128)S(1)}, u32[]{:S(2)}, u32[]{:S(2)}) collective-permute-start(f32[2,3,2,8,16]{4,2,3,1,0:T(2,128)S(1)} %fusion.51), channel_id=1, source_target_pairs={{8,0},{16,8},{24,16},{9,1},{17,9},{25,17},{10,2},{18,10},{26,18},{... | collective-permute-start | bytes 18440 | tf_op jit(solution)/shard_map/ppermute | solution.py:20
  91.1 3.5 %collective-permute-done.11 = f32[2,3,2,8,16]{4,2,3,1,0:T(2,128)S(1)} collective-permute-done((f32[2,3,2,8,16]{4,2,3,1,0:T(2,128)S(1)}, f32[2,3,2,8,16]{4,2,3,1,0:T(2,128)S(1)}, u32[]{:S(2)}, u32[]{:S(2)}) %collective-permute-start.11) | collective-permute-done | bytes 6176 | tf_op jit(solution)/shard_map/ppermute | solution.py:20
  94.8 4.6 %collective-permute-start.12 = (f32[2,3,6,8,2]{4,2,3,1,0:T(8,128)S(1)}, f32[2,3,6,8,2]{4,2,3,1,0:T(8,128)S(1)}, u32[]{:S(2)}, u32[]{:S(2)}) collective-permute-start(f32[2,3,6,8,2]{4,2,3,1,0:T(8,128)S(1)} %get-tuple-element.29), channel_id=1, source_target_pairs={{0,1},{1,2},{2,3},{4,5},{5,6},{6,7},{8,9},{9,10},{10,11},{12,13},{... | collective-permute-start | bytes 6920 | tf_op jit(solution)/shard_map/ppermute | solution.py:18
  99.4 1.9 %collective-permute-start.13 = (f32[2,3,6,8,2]{4,2,3,1,0:T(8,128)S(1)}, f32[2,3,6,8,2]{4,2,3,1,0:T(8,128)S(1)}, u32[]{:S(2)}, u32[]{:S(2)}) collective-permute-start(f32[2,3,6,8,2]{4,2,3,1,0:T(8,128)S(1)} %get-tuple-element.28), channel_id=1, source_target_pairs={{1,0},{2,1},{3,2},{5,4},{6,5},{7,6},{9,8},{10,9},{11,10},{13,12},{... | collective-permute-start | bytes 6920 | tf_op jit(solution)/shard_map/ppermute | solution.py:20
  102.0 4.4 %collective-permute-done.13 = f32[2,3,6,8,2]{4,2,3,1,0:T(8,128)S(1)} collective-permute-done((f32[2,3,6,8,2]{4,2,3,1,0:T(8,128)S(1)}, f32[2,3,6,8,2]{4,2,3,1,0:T(8,128)S(1)}, u32[]{:S(2)}, u32[]{:S(2)}) %collective-permute-start.13) | collective-permute-done | bytes 2336 | tf_op jit(solution)/shard_map/ppermute | solution.py:20
  107.4 2.1 %convolution_bitcast_fusion = f32[2,3,16,32,20]{3,4,2,1,0:T(8,128)S(1)} fusion(f32[2,3,16,8,20]{4,2,3,1,0:T(8,128)S(1)} %convolution_bitcast_fusion.1, f32[8]{0:T(128)S(1)} %multiply_add_fusion.1), kind=kOutput, calls=%fused_computation.23 | convolution fusion | flops 5902336 | bytes 307232 | tf_op jit(solution)/shard_map/hcxjk,yj->hcxyk/dot_general | solution.py:141
  109.4 3.6 %convolution_convert_fusion = bf16[2,3,16,32,128]{4,3,2,1,0:T(8,128)(2,1)} fusion(f32[2,3,16,32,20]{3,4,2,1,0:T(8,128)S(1)} %convolution_bitcast_fusion, f32[20]{0:T(128)S(1)} %multiply_add_fusion), kind=kOutput, calls=%fused_computation.22 | convolution fusion | flops 94806016 | bytes 1032272 | tf_op jit(solution)/shard_map/hcxyk,zk->hcxyz/dot_general | solution.py:142
  (51 shorter events, 10.4 us)
Async XLA Ops:
  1.6 6.2 %collective-permute-start = (f32[2,4,32,128]{3,2,1,0:T(8,128)S(1)}, f32[2,4,32,128]{3,2,1,0:T(8,128)S(1)}, u32[]{:S(2)}, u32[]{:S(2)}) collective-permute-start(f32[2,4,32,128]{3,2,1,0:T(8,128)S(1)} %get-tuple-element.25), channel_id=1, source_target_pairs={{0,8},{8,16},{16,24},{1,9},{9,17},{17,25},{2,10},{10,18},{18,26},{... | collective-permute-start | bytes 393224 | tf_op jit(solution)/shard_map/ppermute | solution.py:18
  5.7 5.7 %collective-permute-start.1 = (f32[2,4,32,128]{3,2,1,0:T(8,128)S(1)}, f32[2,4,32,128]{3,2,1,0:T(8,128)S(1)}, u32[]{:S(2)}, u32[]{:S(2)}) collective-permute-start(f32[2,4,32,128]{3,2,1,0:T(8,128)S(1)} %get-tuple-element.24), channel_id=1, source_target_pairs={{8,0},{16,8},{24,16},{9,1},{17,9},{25,17},{10,2},{18,10},{26,18},{... | collective-permute-start | bytes 393224 | tf_op jit(solution)/shard_map/ppermute | solution.py:20
  11.4 4.7 %collective-permute-start.2 = (f32[2,24,4,128]{3,1,2,0:T(8,128)S(1)}, f32[2,24,4,128]{3,1,2,0:T(8,128)S(1)}, u32[]{:S(2)}, u32[]{:S(2)}) collective-permute-start(f32[2,24,4,128]{3,1,2,0:T(8,128)S(1)} %copy.59), channel_id=1, source_target_pairs={{0,4},{1,5},{2,6},{3,7},{8,12},{9,13},{10,14},{11,15},{16,20},{17,... | collective-permute-start | bytes 294920 | tf_op jit(solution)/shard_map/ppermute | solution.py:18
  14.6 5.4 %collective-permute-start.3 = (f32[2,24,4,128]{3,1,2,0:T(8,128)S(1)}, f32[2,24,4,128]{3,1,2,0:T(8,128)S(1)}, u32[]{:S(2)}, u32[]{:S(2)}) collective-permute-start(f32[2,24,4,128]{3,1,2,0:T(8,128)S(1)} %copy.60), channel_id=1, source_target_pairs={{4,0},{5,1},{6,2},{7,3},{12,8},{13,9},{14,10},{15,11},{20,16},{21,... | collective-permute-start | bytes 294920 | tf_op jit(solution)/shard_map/ppermute | solution.py:20
  20.8 8.9 %collective-permute-start.4 = (f32[2,24,40,4]{2,1,3,0:T(8,128)S(1)}, f32[2,24,40,4]{2,1,3,0:T(8,128)S(1)}, u32[]{:S(2)}, u32[]{:S(2)}) collective-permute-start(f32[2,24,40,4]{2,1,3,0:T(8,128)S(1)} %copy.44), channel_id=1, source_target_pairs={{0,1},{1,2},{2,3},{4,5},{5,6},{6,7},{8,9},{9,10},{10,11},{12,13},{... | collective-permute-start | bytes 92168 | tf_op jit(solution)/shard_map/ppermute | solution.py:18
  27.8 5.9 %collective-permute-start.5 = (f32[2,24,40,4]{2,1,3,0:T(8,128)S(1)}, f32[2,24,40,4]{2,1,3,0:T(8,128)S(1)}, u32[]{:S(2)}, u32[]{:S(2)}) collective-permute-start(f32[2,24,40,4]{2,1,3,0:T(8,128)S(1)} %copy.45), channel_id=1, source_target_pairs={{1,0},{2,1},{3,2},{5,4},{6,5},{7,6},{9,8},{10,9},{11,10},{13,12},{... | collective-permute-start | bytes 92168 | tf_op jit(solution)/shard_map/ppermute | solution.py:20
  58.6 27.9 %copy-start = (f32[2,3,2,8,16]{4,3,2,1,0:T(8,128)S(1)}, f32[2,3,2,8,16]{4,3,2,1,0:T(8,128)}, u32[]{:S(2)}) copy-start(f32[2,3,2,8,16]{4,3,2,1,0:T(8,128)} %param.3) | copy-start | bytes 18436
  59.1 4.7 %collective-permute-start.6 = (f32[2,3,2,8,20]{4,2,3,1,0:T(2,128)S(1)}, f32[2,3,2,8,20]{4,2,3,1,0:T(2,128)S(1)}, u32[]{:S(2)}, u32[]{:S(2)}) collective-permute-start(f32[2,3,2,8,20]{4,2,3,1,0:T(2,128)S(1)} %get-tuple-element.30), channel_id=1, source_target_pairs={{0,8},{8,16},{16,24},{1,9},{9,17},{17,25},{2,10},{10,18},{18,26},{... | collective-permute-start | bytes 23048 | tf_op jit(solution)/shard_map/ppermute | solution.py:18
  62.3 4.8 %collective-permute-start.7 = (f32[2,3,2,8,20]{4,2,3,1,0:T(2,128)S(1)}, f32[2,3,2,8,20]{4,2,3,1,0:T(2,128)S(1)}, u32[]{:S(2)}, u32[]{:S(2)}) collective-permute-start(f32[2,3,2,8,20]{4,2,3,1,0:T(2,128)S(1)} %get-tuple-element.31), channel_id=1, source_target_pairs={{8,0},{16,8},{24,16},{9,1},{17,9},{25,17},{10,2},{18,10},{26,18},{... | collective-permute-start | bytes 23048 | tf_op jit(solution)/shard_map/ppermute | solution.py:20
  67.4 8.0 %collective-permute-start.8 = (f32[2,3,10,8,2]{4,2,3,1,0:T(8,128)S(1)}, f32[2,3,10,8,2]{4,2,3,1,0:T(8,128)S(1)}, u32[]{:S(2)}, u32[]{:S(2)}) collective-permute-start(f32[2,3,10,8,2]{4,2,3,1,0:T(8,128)S(1)} %get-tuple-element.26), channel_id=1, source_target_pairs={{0,1},{1,2},{2,3},{4,5},{5,6},{6,7},{8,9},{9,10},{10,11},{12,13},{... | collective-permute-start | bytes 11528 | tf_op jit(solution)/shard_map/ppermute | solution.py:18
  70.6 9.4 %collective-permute-start.9 = (f32[2,3,10,8,2]{4,2,3,1,0:T(8,128)S(1)}, f32[2,3,10,8,2]{4,2,3,1,0:T(8,128)S(1)}, u32[]{:S(2)}, u32[]{:S(2)}) collective-permute-start(f32[2,3,10,8,2]{4,2,3,1,0:T(8,128)S(1)} %get-tuple-element.27), channel_id=1, source_target_pairs={{1,0},{2,1},{3,2},{5,4},{6,5},{7,6},{9,8},{10,9},{11,10},{13,12},{... | collective-permute-start | bytes 11528 | tf_op jit(solution)/shard_map/ppermute | solution.py:20
  86.6 4.5 %collective-permute-start.10 = (f32[2,3,2,8,16]{4,2,3,1,0:T(2,128)S(1)}, f32[2,3,2,8,16]{4,2,3,1,0:T(2,128)S(1)}, u32[]{:S(2)}, u32[]{:S(2)}) collective-permute-start(f32[2,3,2,8,16]{4,2,3,1,0:T(2,128)S(1)} %fusion.51), channel_id=1, source_target_pairs={{0,8},{8,16},{16,24},{1,9},{9,17},{17,25},{2,10},{10,18},{18,26},{... | collective-permute-start | bytes 18440 | tf_op jit(solution)/shard_map/ppermute | solution.py:18
  89.8 4.8 %collective-permute-start.11 = (f32[2,3,2,8,16]{4,2,3,1,0:T(2,128)S(1)}, f32[2,3,2,8,16]{4,2,3,1,0:T(2,128)S(1)}, u32[]{:S(2)}, u32[]{:S(2)}) collective-permute-start(f32[2,3,2,8,16]{4,2,3,1,0:T(2,128)S(1)} %fusion.51), channel_id=1, source_target_pairs={{8,0},{16,8},{24,16},{9,1},{17,9},{25,17},{10,2},{18,10},{26,18},{... | collective-permute-start | bytes 18440 | tf_op jit(solution)/shard_map/ppermute | solution.py:20
  94.8 7.2 %collective-permute-start.12 = (f32[2,3,6,8,2]{4,2,3,1,0:T(8,128)S(1)}, f32[2,3,6,8,2]{4,2,3,1,0:T(8,128)S(1)}, u32[]{:S(2)}, u32[]{:S(2)}) collective-permute-start(f32[2,3,6,8,2]{4,2,3,1,0:T(8,128)S(1)} %get-tuple-element.29), channel_id=1, source_target_pairs={{0,1},{1,2},{2,3},{4,5},{5,6},{6,7},{8,9},{9,10},{10,11},{12,13},{... | collective-permute-start | bytes 6920 | tf_op jit(solution)/shard_map/ppermute | solution.py:18
  99.4 7.0 %collective-permute-start.13 = (f32[2,3,6,8,2]{4,2,3,1,0:T(8,128)S(1)}, f32[2,3,6,8,2]{4,2,3,1,0:T(8,128)S(1)}, u32[]{:S(2)}, u32[]{:S(2)}) collective-permute-start(f32[2,3,6,8,2]{4,2,3,1,0:T(8,128)S(1)} %get-tuple-element.28), channel_id=1, source_target_pairs={{1,0},{2,1},{3,2},{5,4},{6,5},{7,6},{9,8},{10,9},{11,10},{13,12},{... | collective-permute-start | bytes 6920 | tf_op jit(solution)/shard_map/ppermute | solution.py:20
where the time goes:
time: 114 us; the launch traced here: 113 us
  starting transfers between devices  39.2 us (34%)
  waiting for transfers between devices  29.5 us (26%)
  matrix products  19.8 us (17%)
  other arithmetic  12.7 us (11%)
  blocking collectives  5.6 us (5%)
  local copies, waits for them, and re-layouts  5.12 us (4%)
    ppermute x7, starting transfers between devices, extended_2(): lax.ppermute(tail, axis, [(i, (i + 1) % count) for i in range(ends)])  28 us
    ppermute x7, waiting for transfers between devices, extended_2(): lax.ppermute(head, axis, [((i + 1) % count, i) for i in range(ends)])  25.7 us
    ppermute x7, starting transfers between devices, extended_2(): lax.ppermute(head, axis, [((i + 1) % count, i) for i in range(ends)])  11.2 us
    dot_general x1, matrix products, shards(): along_z = jnp.einsum('hcxyz,zk->hcxyk', pushes, table_z, precision=highest)  6.22 us
    dot_general x1, matrix products, shards(): along_y = jnp.einsum('hcxyk,yj->hcxjk', along_z, table_y, precision=highest)  5.91 us
    psum x1, blocking collectives, shards(): summed = lax.psum(canvas, 'gy')  5.6 us
    add x2, other arithmetic, window_sum(): running + lax.slice_in_dim(values, offset, offset + keep_count, axis=whic...  5 us
    ppermute x7, waiting for transfers between devices, extended_2(): lax.ppermute(tail, axis, [(i, (i + 1) % count) for i in range(ends)])  3.85 us
  transfers between devices with their start and end apart: 14, of which 10 were waited for; matrix products, arithmetic and copies ran while one was open for 2% of the time, Pallas kernels for 0%

commit v1 on v0

--- a/solution.py
+++ b/solution.py
@@ -131,7 +131,7 @@
     whole_rows = block_y * lax.axis_size("gy") + 4
     canvas = jnp.zeros((2, 3, block_x, whole_rows, block_z), jnp.float32)
     canvas = lax.dynamic_update_slice_in_dim(canvas, folded, lax.axis_index("gy") * block_y, 3)
-    summed = lax.psum(canvas, "gy")
+    summed = jnp.sum(lax.all_gather(canvas, "gy"), axis=0)
     descent = summed[:, :, :, 2 : whole_rows - 2, :]
     new_velocity = velocity + step_size * descent
     beside_all = extended_2(new_velocity, (("gx", 2), ("gz", 4)), 2)

time: 114 us -> 111 us (0.974)
  blocking collectives: 5.6 us -> 3.87 us
    psum x1 -> x0, blocking collectives: 5.6 us -> none  [shards(): summed = lax.psum(canvas, 'gy')]
    all_gather x0 -> x1, blocking collectives: none -> 3.87 us  [shards(): summed = jnp.sum(lax.all_gather(canvas, 'gy'), axis=0)]
where the time goes in v1:
time: 111 us
  starting transfers between devices  38.9 us (35%)
  waiting for transfers between devices  29.2 us (26%)
  matrix products  19.8 us (18%)
  other arithmetic  12.8 us (12%)
  local copies, waits for them, and re-layouts  5.12 us (5%)
  blocking collectives  3.87 us (3%)
    ppermute x7, starting transfers between devices, extended_2(): lax.ppermute(tail, axis, [(i, (i + 1) % count) for i in range(ends)])  27.7 us
    ppermute x7, waiting for transfers between devices, extended_2(): lax.ppermute(head, axis, [((i + 1) % count, i) for i in range(ends)])  25.4 us
    ppermute x7, starting transfers between devices, extended_2(): lax.ppermute(head, axis, [((i + 1) % count, i) for i in range(ends)])  11.2 us
    dot_general x1, matrix products, shards(): along_z = jnp.einsum('hcxyz,zk->hcxyk', pushes, table_z, precision=highest)  6.22 us
    dot_general x1, matrix products, shards(): along_y = jnp.einsum('hcxyk,yj->hcxjk', along_z, table_y, precision=highest)  5.91 us
    add x2, other arithmetic, window_sum(): running + lax.slice_in_dim(values, offset, offset + keep_count, axis=whic...  5 us
    all_gather x1, blocking collectives, shards(): summed = jnp.sum(lax.all_gather(canvas, 'gy'), axis=0)  3.87 us
    ppermute x7, waiting for transfers between devices, extended_2(): lax.ppermute(tail, axis, [(i, (i + 1) % count) for i in range(ends)])  3.85 us
  transfers between devices with their start and end apart: 14, of which 10 were waited for; matrix products, arithmetic and copies ran while one was open for 2% of the time, Pallas kernels for 0%

profile of v1, /device:TPU:1, one launch (start us, length us, event | category | flops | bytes accessed | tf_op | source)
XLA Modules:
  0.0 110.8 jit_solution(423475223439617473)
XLA Ops:
  1.6 4.0 %collective-permute-start = (f32[2,4,32,128]{3,2,1,0:T(8,128)S(1)}, f32[2,4,32,128]{3,2,1,0:T(8,128)S(1)}, u32[]{:S(2)}, u32[]{:S(2)}) collective-permute-start(f32[2,4,32,128]{3,2,1,0:T(8,128)S(1)} %get-tuple-element.25), channel_id=1, source_target_pairs={{0,8},{8,16},{16,24},{1,9},{9,17},{17,25},{2,10},{10,18},{18,26},{... | collective-permute-start | bytes 393224 | tf_op jit(solution)/shard_map/ppermute | solution.py:18
  5.7 1.3 %collective-permute-start.1 = (f32[2,4,32,128]{3,2,1,0:T(8,128)S(1)}, f32[2,4,32,128]{3,2,1,0:T(8,128)S(1)}, u32[]{:S(2)}, u32[]{:S(2)}) collective-permute-start(f32[2,4,32,128]{3,2,1,0:T(8,128)S(1)} %get-tuple-element.24), channel_id=1, source_target_pairs={{8,0},{16,8},{24,16},{9,1},{17,9},{25,17},{10,2},{18,10},{26,18},{... | collective-permute-start | bytes 393224 | tf_op jit(solution)/shard_map/ppermute | solution.py:20
  7.8 1.1 constant_dynamic-update-slice_fusion.1
  8.9 2.5 %collective-permute-done.1 = f32[2,4,32,128]{3,2,1,0:T(8,128)S(1)} collective-permute-done((f32[2,4,32,128]{3,2,1,0:T(8,128)S(1)}, f32[2,4,32,128]{3,2,1,0:T(8,128)S(1)}, u32[]{:S(2)}, u32[]{:S(2)}) %collective-permute-start.1) | collective-permute-done | bytes 131104 | tf_op jit(solution)/shard_map/ppermute | solution.py:20
  11.4 3.1 %collective-permute-start.2 = (f32[2,24,4,128]{3,1,2,0:T(8,128)S(1)}, f32[2,24,4,128]{3,1,2,0:T(8,128)S(1)}, u32[]{:S(2)}, u32[]{:S(2)}) collective-permute-start(f32[2,24,4,128]{3,1,2,0:T(8,128)S(1)} %copy.60), channel_id=1, source_target_pairs={{0,4},{1,5},{2,6},{3,7},{8,12},{9,13},{10,14},{11,15},{16,20},{17,... | collective-permute-start | bytes 294920 | tf_op jit(solution)/shard_map/ppermute | solution.py:18
  14.6 1.3 %collective-permute-start.3 = (f32[2,24,4,128]{3,1,2,0:T(8,128)S(1)}, f32[2,24,4,128]{3,1,2,0:T(8,128)S(1)}, u32[]{:S(2)}, u32[]{:S(2)}) collective-permute-start(f32[2,24,4,128]{3,1,2,0:T(8,128)S(1)} %copy.61), channel_id=1, source_target_pairs={{4,0},{5,1},{6,2},{7,3},{12,8},{13,9},{14,10},{15,11},{20,16},{21,... | collective-permute-start | bytes 294920 | tf_op jit(solution)/shard_map/ppermute | solution.py:20
  16.2 3.7 %collective-permute-done.3 = f32[2,24,4,128]{3,1,2,0:T(8,128)S(1)} collective-permute-done((f32[2,24,4,128]{3,1,2,0:T(8,128)S(1)}, f32[2,24,4,128]{3,1,2,0:T(8,128)S(1)}, u32[]{:S(2)}, u32[]{:S(2)}) %collective-permute-start.3) | collective-permute-done | bytes 98336 | tf_op jit(solution)/shard_map/ppermute | solution.py:20
  20.8 6.6 %collective-permute-start.4 = (f32[2,24,40,4]{2,1,3,0:T(8,128)S(1)}, f32[2,24,40,4]{2,1,3,0:T(8,128)S(1)}, u32[]{:S(2)}, u32[]{:S(2)}) collective-permute-start(f32[2,24,40,4]{2,1,3,0:T(8,128)S(1)} %copy.45), channel_id=1, source_target_pairs={{0,1},{1,2},{2,3},{4,5},{5,6},{6,7},{8,9},{9,10},{10,11},{12,13},{... | collective-permute-start | bytes 92168 | tf_op jit(solution)/shard_map/ppermute | solution.py:18
  27.8 1.9 %collective-permute-start.5 = (f32[2,24,40,4]{2,1,3,0:T(8,128)S(1)}, f32[2,24,40,4]{2,1,3,0:T(8,128)S(1)}, u32[]{:S(2)}, u32[]{:S(2)}) collective-permute-start(f32[2,24,40,4]{2,1,3,0:T(8,128)S(1)} %copy.46), channel_id=1, source_target_pairs={{1,0},{2,1},{3,2},{5,4},{6,5},{7,6},{9,8},{10,9},{11,10},{13,12},{... | collective-permute-start | bytes 92168 | tf_op jit(solution)/shard_map/ppermute | solution.py:20
  30.2 3.6 %collective-permute-done.5 = f32[2,24,40,4]{2,1,3,0:T(8,128)S(1)} collective-permute-done((f32[2,24,40,4]{2,1,3,0:T(8,128)S(1)}, f32[2,24,40,4]{2,1,3,0:T(8,128)S(1)}, u32[]{:S(2)}, u32[]{:S(2)}) %collective-permute-start.5) | collective-permute-done | bytes 30752 | tf_op jit(solution)/shard_map/ppermute | solution.py:20
  35.6 1.8 %pad_maximum_fusion = f32[5,24,40,136]{3,2,1,0:T(8,128)S(1)} fusion(f32[1,24,40,136]{3,2,1,0:T(8,128)S(1)} %get-tuple-element.12, f32[1,24,40,136]{3,2,1,0:T(8,128)S(1)} %get-tuple-element.14, f32[1,24,40,136]{3,2,1,0:T(8,128)S(1)} %get-tuple-element.11, f32[2,24,40,4]{3,2,1,0:T(8,128)S(1)} %copy.48, f32[2,24,4,128]{3,2,1,0:T(4,128)S(1)} %copy.44, ...), kind=kLoop, calls=%fused_computation | loop fusion | flops 4569600 | bytes 5222400 | tf_op jit(solution)/shard_map/stack | solution.py:81
  37.4 3.0 %slice_add_fusion = f32[5,16,40,136]{3,2,1,0:T(8,128)S(1)} fusion(f32[5,24,40,136]{3,2,1,0:T(8,128)S(1)} %pad_maximum_fusion), kind=kLoop, calls=%fused_computation.1 | loop fusion | flops 3481600 | bytes 17408000 | tf_op jit(solution)/shard_map/add | solution.py:55
  40.5 2.0 %slice_add_fusion.8 = f32[5,16,32,136]{3,2,1,0:T(8,128)S(1)} fusion(f32[5,16,40,136]{3,2,1,0:T(8,128)S(1)} %slice_add_fusion), kind=kLoop, calls=%fused_computation.9 | loop fusion | flops 2785280 | bytes 13926400 | tf_op jit(solution)/shard_map/add | solution.py:55
  42.4 2.8 %fusion.4 = f32[5,16,32,128]{3,2,1,0:T(8,128)S(1)} fusion(f32[5,16,32,136]{3,2,1,0:T(8,128)S(1)} %slice_add_fusion.8), kind=kLoop, calls=%fused_computation.25 | loop fusion | flops 2949120 | bytes 13107200 | tf_op jit(solution)/shard_map/div | solution.py:91
  46.5 6.2 %fusion = f32[2,3,16,32,20]{3,4,2,1,0:T(8,128)S(1)} fusion(f32[1,3,16,32,128]{4,3,2,1,0:T(8,128)S(1)} %maximum_multiply_fusion.1, f32[1,3,16,32,128]{4,3,2,1,0:T(8,128)S(1)} %maximum_multiply_fusion, f32[20]{0:T(128)S(1)} %multiply_add_fusion), kind=kOutput, calls=%fused_computation.18 | convolution fusion | flops 94806016 | bytes 1818704 | tf_op jit(solution)/shard_map/hcxyz,zk->hcxyk/dot_general | solution.py:123
  52.7 5.9 %convolution_bitcast_fusion.2 = f32[2,3,16,8,20]{4,3,2,1,0:T(8,128)S(1)} fusion(f32[2,3,16,32,20]{3,4,2,1,0:T(8,128)S(1)} %fusion, f32[8]{0:T(128)S(1)} %multiply_add_fusion.1), kind=kOutput, calls=%fused_computation.34 | convolution fusion | flops 5902336 | bytes 307232 | tf_op jit(solution)/shard_map/hcxyk,yj->hcxjk/dot_general | solution.py:124
  59.1 3.2 %collective-permute-start.6 = (f32[2,3,2,8,20]{4,2,3,1,0:T(2,128)S(1)}, f32[2,3,2,8,20]{4,2,3,1,0:T(2,128)S(1)}, u32[]{:S(2)}, u32[]{:S(2)}) collective-permute-start(f32[2,3,2,8,20]{4,2,3,1,0:T(2,128)S(1)} %get-tuple-element.30), channel_id=1, source_target_pairs={{0,8},{8,16},{16,24},{1,9},{9,17},{17,25},{2,10},{10,18},{18,26},{... | collective-permute-start | bytes 23048 | tf_op jit(solution)/shard_map/ppermute | solution.py:18
  62.3 1.5 %collective-permute-start.7 = (f32[2,3,2,8,20]{4,2,3,1,0:T(2,128)S(1)}, f32[2,3,2,8,20]{4,2,3,1,0:T(2,128)S(1)}, u32[]{:S(2)}, u32[]{:S(2)}) collective-permute-start(f32[2,3,2,8,20]{4,2,3,1,0:T(2,128)S(1)} %get-tuple-element.31), channel_id=1, source_target_pairs={{8,0},{16,8},{24,16},{9,1},{17,9},{25,17},{10,2},{18,10},{26,18},{... | collective-permute-start | bytes 23048 | tf_op jit(solution)/shard_map/ppermute | solution.py:20
  63.8 3.3 %collective-permute-done.7 = f32[2,3,2,8,20]{4,2,3,1,0:T(2,128)S(1)} collective-permute-done((f32[2,3,2,8,20]{4,2,3,1,0:T(2,128)S(1)}, f32[2,3,2,8,20]{4,2,3,1,0:T(2,128)S(1)}, u32[]{:S(2)}, u32[]{:S(2)}) %collective-permute-start.7) | collective-permute-done | bytes 7712 | tf_op jit(solution)/shard_map/ppermute | solution.py:20
  67.4 3.3 %collective-permute-start.8 = (f32[2,3,10,8,2]{4,2,3,1,0:T(8,128)S(1)}, f32[2,3,10,8,2]{4,2,3,1,0:T(8,128)S(1)}, u32[]{:S(2)}, u32[]{:S(2)}) collective-permute-start(f32[2,3,10,8,2]{4,2,3,1,0:T(8,128)S(1)} %get-tuple-element.26), channel_id=1, source_target_pairs={{0,1},{1,2},{2,3},{4,5},{5,6},{6,7},{8,9},{9,10},{10,11},{12,13},{... | collective-permute-start | bytes 11528 | tf_op jit(solution)/shard_map/ppermute | solution.py:18
  70.6 1.9 %collective-permute-start.9 = (f32[2,3,10,8,2]{4,2,3,1,0:T(8,128)S(1)}, f32[2,3,10,8,2]{4,2,3,1,0:T(8,128)S(1)}, u32[]{:S(2)}, u32[]{:S(2)}) collective-permute-start(f32[2,3,10,8,2]{4,2,3,1,0:T(8,128)S(1)} %get-tuple-element.27), channel_id=1, source_target_pairs={{1,0},{2,1},{3,2},{5,4},{6,5},{7,6},{9,8},{10,9},{11,10},{13,12},{... | collective-permute-start | bytes 11528 | tf_op jit(solution)/shard_map/ppermute | solution.py:20
  72.6 2.8 %collective-permute-done.8 = f32[2,3,10,8,2]{4,2,3,1,0:T(8,128)S(1)} collective-permute-done((f32[2,3,10,8,2]{4,2,3,1,0:T(8,128)S(1)}, f32[2,3,10,8,2]{4,2,3,1,0:T(8,128)S(1)}, u32[]{:S(2)}, u32[]{:S(2)}) %collective-permute-start.8) | collective-permute-done | bytes 3872 | tf_op jit(solution)/shard_map/ppermute | solution.py:18
  75.3 4.4 %collective-permute-done.9 = f32[2,3,10,8,2]{4,2,3,1,0:T(8,128)S(1)} collective-permute-done((f32[2,3,10,8,2]{4,2,3,1,0:T(8,128)S(1)}, f32[2,3,10,8,2]{4,2,3,1,0:T(8,128)S(1)}, u32[]{:S(2)}, u32[]{:S(2)}) %collective-permute-start.9) | collective-permute-done | bytes 3872 | tf_op jit(solution)/shard_map/ppermute | solution.py:20
  80.6 3.9 %all_gather.7 = f32[2,2,3,2,12,16]{5,3,4,2,1,0:T(2,128)S(1)} all-gather(f32[1,2,3,2,12,16]{5,3,4,2,1,0:T(2,128)S(1)} %copy_dynamic-update-slice_fusion), channel_id=1, replica_groups=mesh['gx'=4,'gy'=2,'gz'=4] {'gy'}, dimensions={0}, use_global_device_ids=true | all-gather | bytes 27648 | tf_op jit(solution)/shard_map/all_gather | solution.py:134
  84.7 3.2 %collective-permute-start.10 = (f32[2,3,2,8,16]{4,2,3,1,0:T(2,128)S(1)}, f32[2,3,2,8,16]{4,2,3,1,0:T(2,128)S(1)}, u32[]{:S(2)}, u32[]{:S(2)}) collective-permute-start(f32[2,3,2,8,16]{4,2,3,1,0:T(2,128)S(1)} %fusion.51), channel_id=1, source_target_pairs={{0,8},{8,16},{16,24},{1,9},{9,17},{17,25},{2,10},{10,18},{18,26},{... | collective-permute-start | bytes 18440 | tf_op jit(solution)/shard_map/ppermute | solution.py:18
  87.9 1.3 %collective-permute-start.11 = (f32[2,3,2,8,16]{4,2,3,1,0:T(2,128)S(1)}, f32[2,3,2,8,16]{4,2,3,1,0:T(2,128)S(1)}, u32[]{:S(2)}, u32[]{:S(2)}) collective-permute-start(f32[2,3,2,8,16]{4,2,3,1,0:T(2,128)S(1)} %fusion.51), channel_id=1, source_target_pairs={{8,0},{16,8},{24,16},{9,1},{17,9},{25,17},{10,2},{18,10},{26,18},{... | collective-permute-start | bytes 18440 | tf_op jit(solution)/shard_map/ppermute | solution.py:20
  89.2 3.5 %collective-permute-done.11 = f32[2,3,2,8,16]{4,2,3,1,0:T(2,128)S(1)} collective-permute-done((f32[2,3,2,8,16]{4,2,3,1,0:T(2,128)S(1)}, f32[2,3,2,8,16]{4,2,3,1,0:T(2,128)S(1)}, u32[]{:S(2)}, u32[]{:S(2)}) %collective-permute-start.11) | collective-permute-done | bytes 6176 | tf_op jit(solution)/shard_map/ppermute | solution.py:20
  92.9 4.3 %collective-permute-start.12 = (f32[2,3,6,8,2]{4,2,3,1,0:T(8,128)S(1)}, f32[2,3,6,8,2]{4,2,3,1,0:T(8,128)S(1)}, u32[]{:S(2)}, u32[]{:S(2)}) collective-permute-start(f32[2,3,6,8,2]{4,2,3,1,0:T(8,128)S(1)} %get-tuple-element.29), channel_id=1, source_target_pairs={{0,1},{1,2},{2,3},{4,5},{5,6},{6,7},{8,9},{9,10},{10,11},{12,13},{... | collective-permute-start | bytes 6920 | tf_op jit(solution)/shard_map/ppermute | solution.py:18
  97.2 1.9 %collective-permute-start.13 = (f32[2,3,6,8,2]{4,2,3,1,0:T(8,128)S(1)}, f32[2,3,6,8,2]{4,2,3,1,0:T(8,128)S(1)}, u32[]{:S(2)}, u32[]{:S(2)}) collective-permute-start(f32[2,3,6,8,2]{4,2,3,1,0:T(8,128)S(1)} %get-tuple-element.28), channel_id=1, source_target_pairs={{1,0},{2,1},{3,2},{5,4},{6,5},{7,6},{9,8},{10,9},{11,10},{13,12},{... | collective-permute-start | bytes 6920 | tf_op jit(solution)/shard_map/ppermute | solution.py:20
  99.8 4.4 %collective-permute-done.13 = f32[2,3,6,8,2]{4,2,3,1,0:T(8,128)S(1)} collective-permute-done((f32[2,3,6,8,2]{4,2,3,1,0:T(8,128)S(1)}, f32[2,3,6,8,2]{4,2,3,1,0:T(8,128)S(1)}, u32[]{:S(2)}, u32[]{:S(2)}) %collective-permute-start.13) | collective-permute-done | bytes 2336 | tf_op jit(solution)/shard_map/ppermute | solution.py:20
  105.1 2.1 %convolution_bitcast_fusion = f32[2,3,16,32,20]{3,4,2,1,0:T(8,128)S(1)} fusion(f32[2,3,16,8,20]{4,2,3,1,0:T(8,128)S(1)} %convolution_bitcast_fusion.1, f32[8]{0:T(128)S(1)} %multiply_add_fusion.1), kind=kOutput, calls=%fused_computation.23 | convolution fusion | flops 5902336 | bytes 307232 | tf_op jit(solution)/shard_map/hcxjk,yj->hcxyk/dot_general | solution.py:141
  107.2 3.6 %convolution_convert_fusion = bf16[2,3,16,32,128]{4,3,2,1,0:T(8,128)(2,1)} fusion(f32[2,3,16,32,20]{3,4,2,1,0:T(8,128)S(1)} %convolution_bitcast_fusion, f32[20]{0:T(128)S(1)} %multiply_add_fusion), kind=kOutput, calls=%fused_computation.22 | convolution fusion | flops 94806016 | bytes 1032272 | tf_op jit(solution)/shard_map/hcxyk,zk->hcxyz/dot_general | solution.py:142
  (52 shorter events, 10.5 us)
Async XLA Ops:
  1.6 6.2 %collective-permute-start = (f32[2,4,32,128]{3,2,1,0:T(8,128)S(1)}, f32[2,4,32,128]{3,2,1,0:T(8,128)S(1)}, u32[]{:S(2)}, u32[]{:S(2)}) collective-permute-start(f32[2,4,32,128]{3,2,1,0:T(8,128)S(1)} %get-tuple-element.25), channel_id=1, source_target_pairs={{0,8},{8,16},{16,24},{1,9},{9,17},{17,25},{2,10},{10,18},{18,26},{... | collective-permute-start | bytes 393224 | tf_op jit(solution)/shard_map/ppermute | solution.py:18
  5.7 5.7 %collective-permute-start.1 = (f32[2,4,32,128]{3,2,1,0:T(8,128)S(1)}, f32[2,4,32,128]{3,2,1,0:T(8,128)S(1)}, u32[]{:S(2)}, u32[]{:S(2)}) collective-permute-start(f32[2,4,32,128]{3,2,1,0:T(8,128)S(1)} %get-tuple-element.24), channel_id=1, source_target_pairs={{8,0},{16,8},{24,16},{9,1},{17,9},{25,17},{10,2},{18,10},{26,18},{... | collective-permute-start | bytes 393224 | tf_op jit(solution)/shard_map/ppermute | solution.py:20
  11.4 4.7 %collective-permute-start.2 = (f32[2,24,4,128]{3,1,2,0:T(8,128)S(1)}, f32[2,24,4,128]{3,1,2,0:T(8,128)S(1)}, u32[]{:S(2)}, u32[]{:S(2)}) collective-permute-start(f32[2,24,4,128]{3,1,2,0:T(8,128)S(1)} %copy.60), channel_id=1, source_target_pairs={{0,4},{1,5},{2,6},{3,7},{8,12},{9,13},{10,14},{11,15},{16,20},{17,... | collective-permute-start | bytes 294920 | tf_op jit(solution)/shard_map/ppermute | solution.py:18
  14.6 5.4 %collective-permute-start.3 = (f32[2,24,4,128]{3,1,2,0:T(8,128)S(1)}, f32[2,24,4,128]{3,1,2,0:T(8,128)S(1)}, u32[]{:S(2)}, u32[]{:S(2)}) collective-permute-start(f32[2,24,4,128]{3,1,2,0:T(8,128)S(1)} %copy.61), channel_id=1, source_target_pairs={{4,0},{5,1},{6,2},{7,3},{12,8},{13,9},{14,10},{15,11},{20,16},{21,... | collective-permute-start | bytes 294920 | tf_op jit(solution)/shard_map/ppermute | solution.py:20
  20.8 8.9 %collective-permute-start.4 = (f32[2,24,40,4]{2,1,3,0:T(8,128)S(1)}, f32[2,24,40,4]{2,1,3,0:T(8,128)S(1)}, u32[]{:S(2)}, u32[]{:S(2)}) collective-permute-start(f32[2,24,40,4]{2,1,3,0:T(8,128)S(1)} %copy.45), channel_id=1, source_target_pairs={{0,1},{1,2},{2,3},{4,5},{5,6},{6,7},{8,9},{9,10},{10,11},{12,13},{... | collective-permute-start | bytes 92168 | tf_op jit(solution)/shard_map/ppermute | solution.py:18
  27.8 5.9 %collective-permute-start.5 = (f32[2,24,40,4]{2,1,3,0:T(8,128)S(1)}, f32[2,24,40,4]{2,1,3,0:T(8,128)S(1)}, u32[]{:S(2)}, u32[]{:S(2)}) collective-permute-start(f32[2,24,40,4]{2,1,3,0:T(8,128)S(1)} %copy.46), channel_id=1, source_target_pairs={{1,0},{2,1},{3,2},{5,4},{6,5},{7,6},{9,8},{10,9},{11,10},{13,12},{... | collective-permute-start | bytes 92168 | tf_op jit(solution)/shard_map/ppermute | solution.py:20
  58.6 26.0 %copy-start = (f32[2,3,2,8,16]{4,3,2,1,0:T(8,128)S(1)}, f32[2,3,2,8,16]{4,3,2,1,0:T(8,128)}, u32[]{:S(2)}) copy-start(f32[2,3,2,8,16]{4,3,2,1,0:T(8,128)} %param.3) | copy-start | bytes 18436
  59.1 4.7 %collective-permute-start.6 = (f32[2,3,2,8,20]{4,2,3,1,0:T(2,128)S(1)}, f32[2,3,2,8,20]{4,2,3,1,0:T(2,128)S(1)}, u32[]{:S(2)}, u32[]{:S(2)}) collective-permute-start(f32[2,3,2,8,20]{4,2,3,1,0:T(2,128)S(1)} %get-tuple-element.30), channel_id=1, source_target_pairs={{0,8},{8,16},{16,24},{1,9},{9,17},{17,25},{2,10},{10,18},{18,26},{... | collective-permute-start | bytes 23048 | tf_op jit(solution)/shard_map/ppermute | solution.py:18
  62.3 4.8 %collective-permute-start.7 = (f32[2,3,2,8,20]{4,2,3,1,0:T(2,128)S(1)}, f32[2,3,2,8,20]{4,2,3,1,0:T(2,128)S(1)}, u32[]{:S(2)}, u32[]{:S(2)}) collective-permute-start(f32[2,3,2,8,20]{4,2,3,1,0:T(2,128)S(1)} %get-tuple-element.31), channel_id=1, source_target_pairs={{8,0},{16,8},{24,16},{9,1},{17,9},{25,17},{10,2},{18,10},{26,18},{... | collective-permute-start | bytes 23048 | tf_op jit(solution)/shard_map/ppermute | solution.py:20
  67.4 8.0 %collective-permute-start.8 = (f32[2,3,10,8,2]{4,2,3,1,0:T(8,128)S(1)}, f32[2,3,10,8,2]{4,2,3,1,0:T(8,128)S(1)}, u32[]{:S(2)}, u32[]{:S(2)}) collective-permute-start(f32[2,3,10,8,2]{4,2,3,1,0:T(8,128)S(1)} %get-tuple-element.26), channel_id=1, source_target_pairs={{0,1},{1,2},{2,3},{4,5},{5,6},{6,7},{8,9},{9,10},{10,11},{12,13},{... | collective-permute-start | bytes 11528 | tf_op jit(solution)/shard_map/ppermute | solution.py:18
  70.6 9.1 %collective-permute-start.9 = (f32[2,3,10,8,2]{4,2,3,1,0:T(8,128)S(1)}, f32[2,3,10,8,2]{4,2,3,1,0:T(8,128)S(1)}, u32[]{:S(2)}, u32[]{:S(2)}) collective-permute-start(f32[2,3,10,8,2]{4,2,3,1,0:T(8,128)S(1)} %get-tuple-element.27), channel_id=1, source_target_pairs={{1,0},{2,1},{3,2},{5,4},{6,5},{7,6},{9,8},{10,9},{11,10},{13,12},{... | collective-permute-start | bytes 11528 | tf_op jit(solution)/shard_map/ppermute | solution.py:20
  84.7 4.5 %collective-permute-start.10 = (f32[2,3,2,8,16]{4,2,3,1,0:T(2,128)S(1)}, f32[2,3,2,8,16]{4,2,3,1,0:T(2,128)S(1)}, u32[]{:S(2)}, u32[]{:S(2)}) collective-permute-start(f32[2,3,2,8,16]{4,2,3,1,0:T(2,128)S(1)} %fusion.51), channel_id=1, source_target_pairs={{0,8},{8,16},{16,24},{1,9},{9,17},{17,25},{2,10},{10,18},{18,26},{... | collective-permute-start | bytes 18440 | tf_op jit(solution)/shard_map/ppermute | solution.py:18
  87.9 4.8 %collective-permute-start.11 = (f32[2,3,2,8,16]{4,2,3,1,0:T(2,128)S(1)}, f32[2,3,2,8,16]{4,2,3,1,0:T(2,128)S(1)}, u32[]{:S(2)}, u32[]{:S(2)}) collective-permute-start(f32[2,3,2,8,16]{4,2,3,1,0:T(2,128)S(1)} %fusion.51), channel_id=1, source_target_pairs={{8,0},{16,8},{24,16},{9,1},{17,9},{25,17},{10,2},{18,10},{26,18},{... | collective-permute-start | bytes 18440 | tf_op jit(solution)/shard_map/ppermute | solution.py:20
  92.9 6.9 %collective-permute-start.12 = (f32[2,3,6,8,2]{4,2,3,1,0:T(8,128)S(1)}, f32[2,3,6,8,2]{4,2,3,1,0:T(8,128)S(1)}, u32[]{:S(2)}, u32[]{:S(2)}) collective-permute-start(f32[2,3,6,8,2]{4,2,3,1,0:T(8,128)S(1)} %get-tuple-element.29), channel_id=1, source_target_pairs={{0,1},{1,2},{2,3},{4,5},{5,6},{6,7},{8,9},{9,10},{10,11},{12,13},{... | collective-permute-start | bytes 6920 | tf_op jit(solution)/shard_map/ppermute | solution.py:18
  97.2 7.0 %collective-permute-start.13 = (f32[2,3,6,8,2]{4,2,3,1,0:T(8,128)S(1)}, f32[2,3,6,8,2]{4,2,3,1,0:T(8,128)S(1)}, u32[]{:S(2)}, u32[]{:S(2)}) collective-permute-start(f32[2,3,6,8,2]{4,2,3,1,0:T(8,128)S(1)} %get-tuple-element.28), channel_id=1, source_target_pairs={{1,0},{2,1},{3,2},{5,4},{6,5},{7,6},{9,8},{10,9},{11,10},{13,12},{... | collective-permute-start | bytes 6920 | tf_op jit(solution)/shard_map/ppermute | solution.py:20
